TPU v7x, 32 devices: a whole 2x2x4 slice. The times are simulated.
32 devices in a mesh: gy: 4 (over y, x), gx: 8 (over z, core).
Axes of the slice: x: 2, y: 2, z: 4, core: 2. Of those that a mesh axis runs over, the one named last changes fastest.
Arguments:
- u_field: float32 [8, 512, 1024], P(None, 'gx', 'gy')
- v_field: float32 [8, 512, 1024], P(None, 'gx', 'gy')
- w_field: float32 [8, 512, 1024], P(None, 'gx', 'gy')
- sep_x: int32 [16], replicated, may hold values from 1 to 128, as said below
- sep_y: int32 [16], replicated, may hold values from 1 to 256, as said below
- sep_z: int32 [16], replicated, may hold values from 1 to 4
Outputs:
- correlation: float32 [3, 16], replicated
Inputs may be any that keep to these rules, and one draw needn't show every extreme that they name: `sep_x`: every separation along x lies in 1 to 128, and 128 is among them in every draw; repeats may occur. `sep_y`: every separation along y lies in 1 to 256, and 256 is among them in every draw; repeats may occur.
All inputs are finite; a program needn't handle non-finite values.
Results may differ from a plain program's by a relative error of at most 0.0003.
Values sent between devices are 32-bit elements; how exact they have to be, the bound alone decides.
A program may use at most 64 MiB of HBM per device.

v0:
```python
import jax
import jax.numpy as jnp
from jax import lax
from jax.sharding import PartitionSpec as P


def from_behind(value, axis, steps):
    count = lax.axis_size(axis)
    pairs = [(source, (source + steps) % count) for source in range(count)]
    return lax.ppermute(value, axis, pairs)


def lag_sums(widened, leading, lag_values, length, axis_dim):

    def one_lag(lag_entry):
        offset, lag_value = lag_entry
        head = lax.dynamic_slice_in_dim(widened, offset, length, axis_dim)
        tail = lax.dynamic_slice_in_dim(widened, offset + lag_value, length, axis_dim)
        return jnp.sum(head * tail)

    return lax.map(one_lag, (leading, lag_values))


def local(u_field, v_field, w_field, sep_x, sep_y, sep_z):
    planes, width_x, width_y = u_field.shape
    u_next = from_behind(u_field, "gx", -1)
    u_after = from_behind(u_next, "gx", -1)
    wide_x = jnp.concatenate([u_field, u_next, u_after], axis=1)
    v_next = from_behind(v_field, "gy", -1)
    wide_y = jnp.concatenate([v_field, v_next], axis=2)
    offset_x = jnp.zeros_like(sep_x)
    offset_y = jnp.zeros_like(sep_y)
    sums_x = lag_sums(wide_x, offset_x, sep_x, width_x, 1)
    sums_y = lag_sums(wide_y, offset_y, sep_y, width_y, 2)
    padded = jnp.concatenate([w_field, jnp.zeros_like(w_field)], axis=0)

    def along_z(lag_value):
        shifted = lax.dynamic_slice_in_dim(padded, lag_value, planes, 0)
        return jnp.sum(w_field * shifted)

    sums_z = lax.map(along_z, sep_z)
    products = jnp.stack([sums_x, sums_y, sums_z], axis=0)
    squares = jnp.stack(
        [jnp.sum(u_field * u_field), jnp.sum(v_field * v_field), jnp.sum(w_field * w_field)]
    )
    totals, energy = lax.psum((products, squares), ("gy", "gx"))
    factor = jnp.float32(planes) / (jnp.float32(planes) - sep_z.astype(jnp.float32))
    row_x = totals[0] / energy[0]
    row_y = totals[1] / energy[1]
    row_z = totals[2] / energy[2] * factor
    return jnp.stack([row_x, row_y, row_z], axis=0)


def solution(mesh):
    return jax.shard_map(
        local,
        mesh=mesh,
        in_specs=(P(None, "gx", "gy"), P(None, "gx", "gy"), P(None, "gx", "gy"), P(), P(), P()),
        out_specs=P(),
        check_vma=False,
    )
```

profile of v0, /device:TPU:0, one launch (start us, length us, event | category | flops | bytes accessed | tf_op | source)
XLA Modules:
  0.0 260.5 jit_solution(6073654299538537000)
XLA Ops:
  0.0 4.5 %collective-permute-start = (f32[8,64,256]{2,1,0:T(8,128)}, f32[8,64,256]{2,1,0:T(8,128)S(1)}, u32[]{:S(2)}, u32[]{:S(2)}) collective-permute-start(f32[8,64,256]{2,1,0:T(8,128)} %param.12), channel_id=1, source_target_pairs={{0,7},{1,0},{2,1},{3,2},{4,3},{5,4},{6,5},{7,6},{8,15},{9,8},{10,9... | collective-permute-start | bytes 1572872 | tf_op jit(solution)/shard_map/ppermute | solution.py:10
  4.5 2.4 collective-permute-start.2
  7.0 1.1 concatenate.11
  8.2 69.8 %while.32 = (s32[]{:T(128)}, f32[16]{0:T(128)S(1)}, s32[16]{0:T(128)S(1)}, f32[16,64,256]{2,1,0:T(8,128)S(1)}, f32[8,64,256]{2,1,0:T(8,128)S(1)}, /*index=5*/s32[]{:T(128)}, s32[]{:T(128)}, s32[]{:T(128)}) while((s32[]{:T(128)}, f32[16]{0:T(128)S(1)}, s32[16]{0:T(128)S(1)}, f32[16,64,256]{2,1,0:T(8,128)S(1)}, f32[8,64,256]{2,1,0:T(8,128)S(1)}, ...), condition=%wide.region_8.9_spmd, body=%wide.region_6.8_spmd.sunk | while | flops 262148 | bytes 1048727 | solution.py:41
  10.9 0.8 multiply_reduce_fusion.11
  15.3 0.8 multiply_reduce_fusion.11
  19.6 0.8 multiply_reduce_fusion.11
  37.1 0.8 multiply_reduce_fusion.11
  41.5 0.8 multiply_reduce_fusion.11
  80.3 2.0 pad_maximum_fusion.4
  82.7 1.2 pad_maximum_fusion.1
  83.9 70.9 %while.31 = (s32[]{:T(128)}, f32[16]{0:T(128)S(1)}, f32[8,64,512]{2,1,0:T(8,128)S(1)}, s32[16]{0:T(128)S(1)}, s32[]{:T(128)}, /*index=5*/s32[]{:T(128)}, s32[]{:T(128)}) while((s32[]{:T(128)}, f32[16]{0:T(128)S(1)}, f32[8,64,512]{2,1,0:T(8,128)S(1)}, s32[16]{0:T(128)S(1)}, s32[]{:T(128)}, /*index=5*/s32[]{:T(128)}, s32[]{:T(128)}) %tuple.58), condition=%wide.region_5.6_spmd, body=%wide.region_3.5_spmd.sunk | while | flops 262148 | bytes 1048719 | solution.py:21
  86.6 0.9 multiply_reduce_fusion.10
  91.1 0.9 multiply_reduce_fusion.10
  95.5 0.9 multiply_reduce_fusion.10
  99.9 0.9 multiply_reduce_fusion.10
  104.4 0.9 multiply_reduce_fusion.10
  108.8 0.9 multiply_reduce_fusion.10
  113.2 0.9 multiply_reduce_fusion.10
  117.6 0.9 multiply_reduce_fusion.10
  122.1 0.9 multiply_reduce_fusion.10
  126.5 0.9 multiply_reduce_fusion.10
  130.9 0.9 multiply_reduce_fusion.10
  135.3 0.9 multiply_reduce_fusion.10
  139.8 0.9 multiply_reduce_fusion.10
  144.2 0.9 multiply_reduce_fusion.10
  148.6 0.9 multiply_reduce_fusion.10
  153.1 0.9 multiply_reduce_fusion.10
  154.7 1.2 pad_maximum_fusion
  155.9 64.5 %while.30 = (s32[]{:T(128)}, f32[16]{0:T(128)S(1)}, f32[8,192,256]{2,1,0:T(8,128)S(1)}, s32[16]{0:T(128)S(1)}, s32[]{:T(128)}, /*index=5*/s32[]{:T(128)}, s32[]{:T(128)}) while((s32[]{:T(128)}, f32[16]{0:T(128)S(1)}, f32[8,192,256]{2,1,0:T(8,128)S(1)}, s32[16]{0:T(128)S(1)}, s32[]{:T(128)}, /*index=5*/s32[]{:T(128)}, s32[]{:T(128)}) %tuple.59), condition=%wide.region_2.3_spmd, body=%wide.region_0.2_spmd.sunk | while | flops 262148 | bytes 1048719 | solution.py:21
  220.5 36.8 %all-reduce.1 = (f32[3,16]{1,0:T(4,128)S(1)}, f32[3]{0:T(128)S(1)}) all-reduce(f32[3,16]{1,0:T(4,128)S(1)} %pad_maximum_fusion.2, f32[3]{0:T(128)S(1)} %pad_maximum_fusion.4), channel_id=1, replica_groups=mesh['gy'=4,'gx'=8] {'gy','gx'}, use_global_device_ids=true, to_apply=%region_9.10 | all-reduce | flops 51 | bytes 408 | tf_op jit(solution)/shard_map/psum | solution.py:46
  258.7 1.2 slice_divide_fusion.1
  (149 shorter events, 94.0 us)
Async XLA Ops:
  0.0 8.1 %copy-start = (f32[8,64,256]{2,1,0:T(8,128)S(1)}, f32[8,64,256]{2,1,0:T(8,128)}, u32[]{:S(2)}) copy-start(f32[8,64,256]{2,1,0:T(8,128)} %param.14) | copy-start | bytes 1572868
  0.0 8.1 %copy-start.3 = (s32[16]{0:T(128)S(1)}, s32[16]{0:T(128)}, u32[]{:S(2)}) copy-start(s32[16]{0:T(128)} %param.17) | copy-start | bytes 196
  0.0 82.3 %collective-permute-start = (f32[8,64,256]{2,1,0:T(8,128)}, f32[8,64,256]{2,1,0:T(8,128)S(1)}, u32[]{:S(2)}, u32[]{:S(2)}) collective-permute-start(f32[8,64,256]{2,1,0:T(8,128)} %param.12), channel_id=1, source_target_pairs={{0,7},{1,0},{2,1},{3,2},{4,3},{5,4},{6,5},{7,6},{8,15},{9,8},{10,9... | collective-permute-start | bytes 1572872 | tf_op jit(solution)/shard_map/ppermute | solution.py:10
  4.5 78.2 %collective-permute-start.2 = (f32[8,64,256]{2,1,0:T(8,128)}, f32[8,64,256]{2,1,0:T(8,128)}, u32[]{:S(2)}, u32[]{:S(2)}) collective-permute-start(f32[8,64,256]{2,1,0:T(8,128)} %param.13), channel_id=1, source_target_pairs={{0,24},{8,0},{16,8},{24,16},{1,25},{9,1},{17,9},{25,17},{2,26},{10... | collective-permute-start | bytes 1572872 | tf_op jit(solution)/shard_map/ppermute | solution.py:10
  8.1 69.9 %copy-start.1 = (f32[8,64,256]{2,1,0:T(8,128)S(1)}, f32[8,64,256]{2,1,0:T(8,128)}, u32[]{:S(2)}) copy-start(f32[8,64,256]{2,1,0:T(8,128)} %param.13) | copy-start | bytes 1572868
  8.1 71.4 %copy-start.2 = (f32[8,64,256]{2,1,0:T(8,128)S(1)}, f32[8,64,256]{2,1,0:T(8,128)}, u32[]{:S(2)}) copy-start(f32[8,64,256]{2,1,0:T(8,128)} %param.12) | copy-start | bytes 1572868
  78.7 5.2 %copy-start.4 = (s32[16]{0:T(128)S(1)}, s32[16]{0:T(128)}, u32[]{:S(2)}) copy-start(s32[16]{0:T(128)} %param.16) | copy-start | bytes 196
  82.3 72.4 %collective-permute-start.1 = (f32[8,64,256]{2,1,0:T(8,128)S(1)}, f32[8,64,256]{2,1,0:T(8,128)}, u32[]{:S(2)}, u32[]{:S(2)}) collective-permute-start(f32[8,64,256]{2,1,0:T(8,128)S(1)} %collective-permute-done), channel_id=1, source_target_pairs={{0,7},{1,0},{2,1},{3,2},{4,3},{5,4},{6,5},{7,6},{8,15},{9,8},{10,9... | collective-permute-start | bytes 1572872 | tf_op jit(solution)/shard_map/ppermute | solution.py:10
  154.7 1.2 copy-start.5
where the time goes:
time: 264 us; the launch traced here: 260 us
  loops' own time  97.6 us (37%)
  local copies, waits for them, and re-layouts  70.1 us (27%)
  other arithmetic  48.5 us (18%)
  blocking collectives  36.8 us (14%)
  starting transfers between devices  7.36 us (3%)
    another operation x2, loops' own time, lag_sums(): return lax.map(one_lag, (leading, lag_values))  64.4 us
    dynamic_update_slice x48, local copies, waits for them, and re-layouts, lag_sums(): return lax.map(one_lag, (leading, lag_values))  37.7 us
    psum x1, blocking collectives, local(): totals, energy = lax.psum((products, squares), ('gy', 'gx'))  36.8 us
    another operation x1, loops' own time, local(): sums_z = lax.map(along_z, sep_z)  33.3 us
    dynamic_slice x48, local copies, waits for them, and re-layouts, lag_sums(): return lax.map(one_lag, (leading, lag_values))  30.6 us
    reduce_sum x32, other arithmetic, one_lag(): return jnp.sum(head * tail)  26.2 us
    reduce_sum x16, other arithmetic, along_z(): return jnp.sum(w_field * shifted)  13.1 us
    ppermute x3, starting transfers between devices, from_behind(): return lax.ppermute(value, axis, pairs)  7.36 us
  transfers between devices with their start and end apart: 3, of which 0 were waited for; matrix products, arithmetic and copies ran while one was open for 31% of the time, Pallas kernels for 0%

commit v1 on v0

v1 whole, which is shorter than its diff:
```python
import functools

import jax
import jax.numpy as jnp
from jax import lax
from jax.experimental import pallas as pl
from jax.experimental.pallas import tpu as pltpu
from jax.sharding import PartitionSpec as P

MESH = pl.DeviceIdType.MESH
LANES = 128
FIELD_LANES = 32


def split(value):
    high = value.astype(jnp.bfloat16)
    low = (value - high.astype(jnp.float32)).astype(jnp.bfloat16)
    return high, low


def product(left, right, dims):
    dot = functools.partial(
        lax.dot_general, dimension_numbers=(dims, ((), ())), preferred_element_type=jnp.float32
    )
    return dot(left[0], right[0]) + (dot(left[0], right[1]) + dot(left[1], right[0]))


def diagonal_sums(gram, largest):
    rows = gram.shape[0]
    window = largest + LANES
    folded = gram[:LANES, :window]
    for start in range(LANES, rows, LANES):
        folded = folded + gram[start : start + LANES, start : start + window]
    total = folded[:8]
    for start in range(8, LANES, 8):
        total = total + pltpu.roll(folded[start : start + 8], window - start, 1)
    row = lax.broadcasted_iota(jnp.int32, total.shape, 0)
    for bit in (1, 2, 4):
        total = jnp.where((row & bit) != 0, pltpu.roll(total, window - bit, 1), total)
    return total


def kernel(
    n_gx, n_gy,
    u_hbm, v_hbm, w_hbm, sep_x_hbm, sep_y_hbm, sep_z_hbm, out_ref,
    u_own, v_own, w_own, u_wide, v_wide, sep_s, gx_rows, gy_rows,
    load_sem, sep_sem, place_sem, u_send, u_recv, d_send, d_recv, v_send, v_recv,
    gx_send, gx_recv, gy_send, gy_recv,
):
    planes, width_x, width_y = u_own.shape
    seps = sep_s.shape[1]
    quarter, half = planes // 4, planes // 2
    gx, gy = lax.axis_index("gx"), lax.axis_index("gy")
    core, parity = lax.rem(gx, 2), lax.rem(gy, 2)
    chip_first = gx - core

    load_u = pltpu.make_async_copy(u_hbm, u_own, load_sem.at[0])
    load_v = pltpu.make_async_copy(v_hbm, v_own, load_sem.at[1])
    load_w = pltpu.make_async_copy(w_hbm, w_own, load_sem.at[2])
    load_u.start()
    load_v.start()

    barrier = pltpu.get_barrier_semaphore()
    for step in range(1, n_gx):
        pl.semaphore_signal(
            barrier, inc=1, device_id={"gx": lax.rem(gx + step, n_gx)}, device_id_type=MESH
        )
    for step in range(1, n_gy):
        pl.semaphore_signal(
            barrier, inc=1, device_id={"gy": lax.rem(gy + step, n_gy)}, device_id_type=MESH
        )
    load_w.start()
    sep_loads = [
        pltpu.make_async_copy(ref, sep_s.at[index], sep_sem.at[index])
        for index, ref in enumerate((sep_x_hbm, sep_y_hbm, sep_z_hbm))
    ]
    places = []
    for side in range(2):
        places.append(pltpu.make_async_copy(
            u_hbm.at[pl.ds(half * side + quarter * core, quarter)],
            u_wide.at[side, :, 2 * side + core],
            place_sem.at[side],
        ))
    places.append(pltpu.make_async_copy(
        v_hbm.at[pl.ds(half * parity, half)], v_wide.at[2 * parity], place_sem.at[2]
    ))
    for copy in places + sep_loads:
        copy.start()

    u_copies = []
    for item in range(quarter):
        for other in range(2):
            for side in range(2):
                chip = lax.rem(chip_first + (n_gx - 2 if side == 0 else 2), n_gx)
                u_copies.append(pltpu.make_async_remote_copy(
                    src_ref=u_own.at[half * side + quarter * other + item],
                    dst_ref=u_wide.at[side, item, (2 if side == 0 else 0) + core],
                    send_sem=u_send.at[side, item, other],
                    recv_sem=u_recv.at[side, item, core],
                    device_id={"gx": chip + other},
                    device_id_type=MESH,
                ))
    d_copies = []
    for side in range(2):
        d_copies.append(pltpu.make_async_remote_copy(
            src_ref=u_own.at[pl.ds(half * side + quarter * (1 - core), quarter)],
            dst_ref=u_wide.at[side, :, 2 * side + core],
            send_sem=d_send.at[side],
            recv_sem=d_recv.at[side],
            device_id={"gx": chip_first + 1 - core},
            device_id_type=MESH,
        ))
    near = gy + 1 - 2 * parity
    far = lax.rem(gy + n_gy - 2 + 4 * parity, n_gy)
    v_copies = []
    for item in range(half):
        v_copies.append(pltpu.make_async_remote_copy(
            src_ref=v_own.at[half * (1 - parity) + item],
            dst_ref=v_wide.at[1, item],
            send_sem=v_send.at[0, item],
            recv_sem=v_recv.at[0, item],
            device_id={"gy": near},
            device_id_type=MESH,
        ))
        v_copies.append(pltpu.make_async_remote_copy(
            src_ref=v_own.at[half * parity + item],
            dst_ref=v_wide.at[2 - 2 * parity, item],
            send_sem=v_send.at[1, item],
            recv_sem=v_recv.at[1, item],
            device_id={"gy": far},
            device_id_type=MESH,
        ))

    load_u.wait()
    load_v.wait()
    pl.semaphore_wait(barrier, n_gx + n_gy - 2)
    for copy in u_copies + v_copies + d_copies:
        copy.start()

    for copy in sep_loads:
        copy.wait()
    lane = lax.broadcasted_iota(jnp.int32, (1, LANES), 1)
    lag_row = jnp.full((1, LANES), -1, jnp.int32)
    for field in range(3):
        for index in range(seps):
            lag_row = jnp.where(lane == FIELD_LANES * field + index, sep_s[field, index], lag_row)
        lag_row = jnp.where(lane == FIELD_LANES * field + seps, 0, lag_row)

    def picker(field, lags):
        of_field = (lane >= FIELD_LANES * field) & (lane < FIELD_LANES * (field + 1))
        wanted = jnp.where(of_field, lag_row, -1)
        lag = lax.broadcasted_iota(jnp.int32, (lags, LANES), 0)
        return jnp.where(lag == wanted, 1.0, 0.0).astype(jnp.float32)

    def pick(sums, field):
        return jnp.dot(
            sums, picker(field, sums.shape[1]),
            precision=lax.Precision.HIGHEST, preferred_element_type=jnp.float32,
        )

    load_w.wait()
    lags_z = half + 1
    tile_rows = 8

    def z_step(index, carry):
        start = pl.multiple_of(index * tile_rows, tile_rows)
        rows = [w_own[plane, pl.ds(start, tile_rows), :] for plane in range(planes)]
        return tuple(
            carry[lag] + sum(rows[plane] * rows[plane + lag] for plane in range(planes - lag))
            for lag in range(lags_z)
        )

    zero = jnp.zeros((tile_rows, width_y), jnp.float32)
    z_sums = lax.fori_loop(0, width_x // tile_rows, z_step, (zero,) * lags_z)
    row_z = jnp.zeros((1, LANES), jnp.float32)
    for lag in range(lags_z):
        row_z = jnp.where(lag_row == lag, jnp.sum(z_sums[lag]), row_z)
    row_z = jnp.where((lane >= 2 * FIELD_LANES) & (lane < 3 * FIELD_LANES), row_z, 0.0)

    for copy in places:
        copy.wait()
    for copy in v_copies:
        copy.wait_recv()
    cells = half * width_x
    wide = v_wide[...].reshape(3 * cells, width_y)
    high, low = split(wide)
    left = (high[: 2 * cells], low[: 2 * cells])
    gram_0 = product(left, left, ((0,), (0,)))
    gram_1 = product(left, (high[cells:], low[cells:]), ((0,), (0,)))
    gram_y = jnp.concatenate([gram_0, gram_1], axis=1)
    part = pick(diagonal_sums(gram_y, width_y), 1)

    for copy in d_copies:
        copy.wait_recv()
    gram_x = None
    for item in range(quarter):
        for side in range(2):
            for sender in range(2):
                slot = (2 if side == 0 else 0) + sender
                pltpu.make_async_remote_copy(
                    src_ref=u_own.at[0],
                    dst_ref=u_wide.at[side, item, slot],
                    send_sem=u_send.at[side, item, sender],
                    recv_sem=u_recv.at[side, item, sender],
                    device_id={"gx": chip_first + 1 - core},
                    device_id_type=MESH,
                ).wait_recv()
            pair = split(u_wide[side, item].reshape(4 * width_x, width_y))
            lower = (pair[0][: 2 * width_x], pair[1][: 2 * width_x])
            term = product(lower, pair, ((1,), (1,)))
            gram_x = term if gram_x is None else gram_x + term
    part = part + pick(diagonal_sums(gram_x, 2 * width_x), 0)
    mine = jnp.sum(part, axis=0, keepdims=True) + row_z

    def all_sum(value, rows_ref, send_sem, recv_sem, axis, me, count):
        rows_ref[me] = value
        copies = []
        for step in range(1, count):
            copies.append(pltpu.make_async_remote_copy(
                src_ref=rows_ref.at[me],
                dst_ref=rows_ref.at[me],
                send_sem=send_sem.at[step],
                recv_sem=recv_sem.at[step],
                device_id={axis: lax.rem(me + step, count)},
                device_id_type=MESH,
            ))
        for copy in copies:
            copy.start()
        for copy in copies:
            copy.wait_recv()
        total = rows_ref[0]
        for index in range(1, count):
            total = total + rows_ref[index]
        return total, copies

    total, copies_gx = all_sum(mine, gx_rows, gx_send, gx_recv, "gx", gx, n_gx)
    total, copies_gy = all_sum(total, gy_rows, gy_send, gy_recv, "gy", gy, n_gy)

    for field in range(3):
        base = FIELD_LANES * field
        row = total[:, base : base + seps] / total[:, base + seps : base + seps + 1]
        if field == 2:
            lag = lag_row[:, base : base + seps].astype(jnp.float32)
            row = row * (jnp.float32(planes) / (jnp.float32(planes) - lag))
        out_ref[field : field + 1, :] = row

    for copy in u_copies + v_copies + d_copies + copies_gx + copies_gy:
        copy.wait_send()


def local(n_gx, n_gy, u_field, v_field, w_field, sep_x, sep_y, sep_z):
    planes, width_x, width_y = u_field.shape
    quarter, half = planes // 4, planes // 2
    seps = sep_x.shape[0]
    dma = pltpu.SemaphoreType.DMA
    block = (planes, width_x, width_y)
    return pl.pallas_call(
        functools.partial(kernel, n_gx, n_gy),
        out_shape=jax.ShapeDtypeStruct((3, seps), jnp.float32),
        in_specs=[pl.BlockSpec(memory_space=pl.ANY)] * 6,
        out_specs=pl.BlockSpec(memory_space=pltpu.VMEM),
        scratch_shapes=[
            pltpu.VMEM(block, jnp.float32),
            pltpu.VMEM(block, jnp.float32),
            pltpu.VMEM(block, jnp.float32),
            pltpu.VMEM((2, quarter, 4, width_x, width_y), jnp.float32),
            pltpu.VMEM((3, half, width_x, width_y), jnp.float32),
            pltpu.SMEM((3, seps), jnp.int32),
            pltpu.VMEM((n_gx, 1, LANES), jnp.float32),
            pltpu.VMEM((n_gy, 1, LANES), jnp.float32),
            dma((3,)),
            dma((3,)),
            dma((3,)),
            dma((2, quarter, 2)),
            dma((2, quarter, 2)),
            dma((2,)),
            dma((2,)),
            dma((2, half)),
            dma((2, half)),
            dma((n_gx,)),
            dma((n_gx,)),
            dma((n_gy,)),
            dma((n_gy,)),
        ],
        compiler_params=pltpu.CompilerParams(collective_id=0, has_side_effects=True),
    )(u_field, v_field, w_field, sep_x, sep_y, sep_z)


def solution(mesh):
    return jax.shard_map(
        functools.partial(local, mesh.shape["gx"], mesh.shape["gy"]),
        mesh=mesh,
        in_specs=(P(None, "gx", "gy"), P(None, "gx", "gy"), P(None, "gx", "gy"), P(), P(), P()),
        out_specs=P(),
        check_vma=False,
    )
```

time: 264 us -> 29.1 us (0.11); the launches traced: 260 us -> 28.9 us
  loops' own time: 97.6 us -> 0 us
  local copies, waits for them, and re-layouts: 70.1 us -> 1.26 us
  other arithmetic: 48.5 us -> 0 us
  blocking collectives: 36.8 us -> 0 us
  Pallas kernels: 0 us -> 27.6 us
  starting transfers between devices: 7.36 us -> 0 us
    another operation x3 -> x0, loops' own time: 97.6 us -> none  [the longest x2 64.4 us: lag_sums(): return lax.map(one_lag, (leading, lag_values))]
    reduce_sum x51 -> x0, other arithmetic: 41.7 us -> none  [the longest x32 26.2 us: one_lag(): return jnp.sum(head * tail)]
    dynamic_update_slice x48 -> x0, local copies, waits for them, and re-layouts: 37.7 us -> none  [lag_sums(): return lax.map(one_lag, (leading, lag_values))]
    psum x1 -> x0, blocking collectives: 36.8 us -> none  [local(): totals, energy = lax.psum((products, squares), ('gy', 'gx'))]
    dynamic_slice x48 -> x0, local copies, waits for them, and re-layouts: 30.6 us -> none  [lag_sums(): return lax.map(one_lag, (leading, lag_values))]
    pallas_call x0 -> x1, Pallas kernels: none -> 27.6 us  [local(): pl.pallas_call(functools.partial(kernel, n_gx, n_gy), out_shape=jax.Shape...]
    ppermute x3 -> x0, starting transfers between devices: 7.36 us -> none  [from_behind(): return lax.ppermute(value, axis, pairs)]
    another operation x4 -> x0, other arithmetic: 3.26 us -> none  [the longest x1 1.96 us: local(): jnp.stack([jnp.sum(u_field * u_field), jnp.sum(v_field * v_field), jnp.su...]
  transfers between devices with their start and end apart: 3 -> 0, of which waited for: 0 -> 0; matrix products, arithmetic and copies ran while one was open for 31% -> 0% of each run, Pallas kernels for 0% -> 0%
where the time goes in v1:
time: 29.1 us; the launch traced here: 28.9 us
  Pallas kernels  27.6 us (95%)
  local copies, waits for them, and re-layouts  1.26 us (4%)
    pallas_call x1, Pallas kernels, local(): pl.pallas_call(functools.partial(kernel, n_gx, n_gy), out_shape=jax.Shape...  27.6 us
    unnamed x1, local copies, waits for them, and re-layouts  1.26 us

profile of v1, /device:TPU:0, one launch (start us, length us, event | category | flops | bytes accessed | tf_op | source)
XLA Modules:
  0.0 28.9 jit_solution(2720198077110735651)
XLA Ops:
  0.0 27.6 %shard_map.64 = f32[3,16]{1,0:T(4,128)} custom-call(f32[8,64,256]{2,1,0:T(8,128)} %u_hbm.1, f32[8,64,256]{2,1,0:T(8,128)} %v_hbm.1, f32[8,64,256]{2,1,0:T(8,128)} %w_hbm.1, s32[16]{0:T(128)} %sep_x_hbm.1, s32[16]{0:T(128)} %sep_y_hbm.1, s32[16]{0:T(128)} %sep_z_hbm.1), custom_call_target="tpu_custom_call" | custom-call | tf_op jit(solution)/shard_map/pallas_call | solution.py:257
  27.6 1.3 %copy.8 = f32[3,16]{1,0:T(4,128)} copy(f32[3,16]{1,0:T(4,128)} %shard_map.64) | data formatting | bytes 384

commit v2 on v1

--- a/solution.py
+++ b/solution.py
@@ -43,9 +43,9 @@
 def kernel(
     n_gx, n_gy,
     u_hbm, v_hbm, w_hbm, sep_x_hbm, sep_y_hbm, sep_z_hbm, out_ref,
-    u_own, v_own, w_own, u_wide, v_wide, sep_s, gx_rows, gy_rows,
+    u_own, v_own, w_own, u_wide, v_wide, sep_s, rows,
     load_sem, sep_sem, place_sem, u_send, u_recv, d_send, d_recv, v_send, v_recv,
-    gx_send, gx_recv, gy_send, gy_recv,
+    row_sem, line_sem, pair_sem,
 ):
     planes, width_x, width_y = u_own.shape
     seps = sep_s.shape[1]
@@ -60,15 +60,29 @@
     load_u.start()
     load_v.start()
 
+    chip, chips = gx // 2, n_gx // 2
+    first, last = chip == 0, chip == chips - 1
+    near = gy + 1 - 2 * parity
+    far_to = lax.rem(gy + n_gy - 2 + 4 * parity, n_gy)
+    far_from = lax.rem(gy + n_gy + 2 - 4 * parity, n_gy)
     barrier = pltpu.get_barrier_semaphore()
-    for step in range(1, n_gx):
-        pl.semaphore_signal(
-            barrier, inc=1, device_id={"gx": lax.rem(gx + step, n_gx)}, device_id_type=MESH
-        )
-    for step in range(1, n_gy):
-        pl.semaphore_signal(
-            barrier, inc=1, device_id={"gy": lax.rem(gy + step, n_gy)}, device_id_type=MESH
-        )
+
+    def greet(semaphore, **device):
+        pl.semaphore_signal(semaphore, inc=1, device_id=device, device_id_type=MESH)
+
+    @pl.when(~first)
+    def _():
+        greet(barrier, gx=chip_first - 2)
+        greet(barrier, gx=chip_first - 1)
+
+    @pl.when(~last)
+    def _():
+        greet(barrier, gx=chip_first + 2)
+        greet(barrier, gx=chip_first + 3)
+
+    greet(barrier, gx=chip_first + 1 - core)
+    greet(barrier, gy=near)
+    greet(barrier, gy=far_from)
     load_w.start()
     sep_loads = [
         pltpu.make_async_copy(ref, sep_s.at[index], sep_sem.at[index])
@@ -87,17 +101,17 @@
     for copy in places + sep_loads:
         copy.start()
 
-    u_copies = []
+    u_copies = {}
     for item in range(quarter):
         for other in range(2):
             for side in range(2):
-                chip = lax.rem(chip_first + (n_gx - 2 if side == 0 else 2), n_gx)
-                u_copies.append(pltpu.make_async_remote_copy(
+                target = lax.rem(chip_first + (n_gx - 2 if side == 0 else 2), n_gx)
+                u_copies[side, item, other] = (pltpu.make_async_remote_copy(
                     src_ref=u_own.at[half * side + quarter * other + item],
                     dst_ref=u_wide.at[side, item, (2 if side == 0 else 0) + core],
                     send_sem=u_send.at[side, item, other],
                     recv_sem=u_recv.at[side, item, core],
-                    device_id={"gx": chip + other},
+                    device_id={"gx": target + other},
                     device_id_type=MESH,
                 ))
     d_copies = []
@@ -110,8 +124,6 @@
             device_id={"gx": chip_first + 1 - core},
             device_id_type=MESH,
         ))
-    near = gy + 1 - 2 * parity
-    far = lax.rem(gy + n_gy - 2 + 4 * parity, n_gy)
     v_copies = []
     for item in range(half):
         v_copies.append(pltpu.make_async_remote_copy(
@@ -127,15 +139,65 @@
             dst_ref=v_wide.at[2 - 2 * parity, item],
             send_sem=v_send.at[1, item],
             recv_sem=v_recv.at[1, item],
-            device_id={"gy": far},
+            device_id={"gy": far_to},
             device_id_type=MESH,
         ))
 
     load_u.wait()
     load_v.wait()
-    pl.semaphore_wait(barrier, n_gx + n_gy - 2)
-    for copy in u_copies + v_copies + d_copies:
+    inner = jnp.where(first, 0, 2) + jnp.where(last, 0, 2)
+    pl.semaphore_wait(barrier, inner + 3)
+
+    def start_u(side, items, at_end):
+        wraps = first if side == 0 else last
+
+        @pl.when(wraps if at_end else ~wraps)
+        def _():
+            for item in items:
+                for other in range(2):
+                    u_copies[side, item, other].start()
+
+    for side in range(2):
+        start_u(side, range(1), False)
+    for copy in v_copies + d_copies:
         copy.start()
+
+    up, down = line_sem.at[0], line_sem.at[1]
+
+    @pl.when(chip == 1)
+    def _():
+        greet(up, gx=gx + 2)
+
+    @pl.when(chip == chips - 2)
+    def _():
+        greet(down, gx=gx - 2)
+
+    @pl.when(chip >= 2)
+    def _():
+        pl.semaphore_wait(up, 1)
+
+    @pl.when((chip >= 2) & (chip <= chips - 2))
+    def _():
+        greet(up, gx=gx + 2)
+
+    @pl.when(chip <= chips - 3)
+    def _():
+        pl.semaphore_wait(down, 1)
+
+    @pl.when((chip >= 1) & (chip <= chips - 3))
+    def _():
+        greet(down, gx=gx - 2)
+
+    for side in range(2):
+        start_u(side, range(quarter), True)
+    for side in range(2):
+        start_u(side, range(1, quarter), False)
+
+    greet(pair_sem.at[0], gy=near)
+    pl.semaphore_wait(pair_sem.at[0], 1)
+    for hop in range(1, n_gy // 2):
+        greet(pair_sem.at[hop], gy=far_from)
+        pl.semaphore_wait(pair_sem.at[hop], 1)
 
     for copy in sep_loads:
         copy.wait()
@@ -150,13 +212,17 @@
         of_field = (lane >= FIELD_LANES * field) & (lane < FIELD_LANES * (field + 1))
         wanted = jnp.where(of_field, lag_row, -1)
         lag = lax.broadcasted_iota(jnp.int32, (lags, LANES), 0)
-        return jnp.where(lag == wanted, 1.0, 0.0).astype(jnp.float32)
-
-    def pick(sums, field):
-        return jnp.dot(
-            sums, picker(field, sums.shape[1]),
-            precision=lax.Precision.HIGHEST, preferred_element_type=jnp.float32,
-        )
+        return jnp.where(lag == wanted, 1.0, 0.0).astype(jnp.bfloat16)
+
+    pick_x = picker(0, 2 * width_x + LANES)
+    pick_y = picker(1, width_y + LANES)
+
+    def pick(sums, chosen):
+        high = sums.astype(jnp.bfloat16).astype(jnp.float32)
+        middle = (sums - high).astype(jnp.bfloat16).astype(jnp.float32)
+        low = (sums - high) - middle
+        parts = jnp.concatenate([high, middle, low], axis=0).astype(jnp.bfloat16)
+        return jnp.dot(parts, chosen, preferred_element_type=jnp.float32)
 
     load_w.wait()
     lags_z = half + 1
@@ -188,7 +254,7 @@
     gram_0 = product(left, left, ((0,), (0,)))
     gram_1 = product(left, (high[cells:], low[cells:]), ((0,), (0,)))
     gram_y = jnp.concatenate([gram_0, gram_1], axis=1)
-    part = pick(diagonal_sums(gram_y, width_y), 1)
+    part = pick(diagonal_sums(gram_y, width_y), pick_y)
 
     for copy in d_copies:
         copy.wait_recv()
@@ -209,32 +275,39 @@
             lower = (pair[0][: 2 * width_x], pair[1][: 2 * width_x])
             term = product(lower, pair, ((1,), (1,)))
             gram_x = term if gram_x is None else gram_x + term
-    part = part + pick(diagonal_sums(gram_x, 2 * width_x), 0)
+    part = part + pick(diagonal_sums(gram_x, 2 * width_x), pick_x)
     mine = jnp.sum(part, axis=0, keepdims=True) + row_z
 
-    def all_sum(value, rows_ref, send_sem, recv_sem, axis, me, count):
-        rows_ref[me] = value
-        copies = []
+    count = n_gx * n_gy
+    me = gx * n_gy + gy
+    rows[me] = mine
+
+    def to_device(step):
+        peer = lax.rem(me + step, count)
+        return pltpu.make_async_remote_copy(
+            src_ref=rows.at[me],
+            dst_ref=rows.at[me],
+            send_sem=row_sem.at[0],
+            recv_sem=row_sem.at[1],
+            device_id={"gx": peer // n_gy, "gy": lax.rem(peer, n_gy)},
+            device_id_type=MESH,
+        )
+
+    if count <= 64:
         for step in range(1, count):
-            copies.append(pltpu.make_async_remote_copy(
-                src_ref=rows_ref.at[me],
-                dst_ref=rows_ref.at[me],
-                send_sem=send_sem.at[step],
-                recv_sem=recv_sem.at[step],
-                device_id={axis: lax.rem(me + step, count)},
-                device_id_type=MESH,
-            ))
-        for copy in copies:
-            copy.start()
-        for copy in copies:
-            copy.wait_recv()
-        total = rows_ref[0]
-        for index in range(1, count):
-            total = total + rows_ref[index]
-        return total, copies
-
-    total, copies_gx = all_sum(mine, gx_rows, gx_send, gx_recv, "gx", gx, n_gx)
-    total, copies_gy = all_sum(total, gy_rows, gy_send, gy_recv, "gy", gy, n_gy)
+            to_device(step).start()
+    else:
+        lax.fori_loop(1, count, lambda step, _: to_device(step).start(), None)
+    all_rows = pltpu.make_async_remote_copy(
+        src_ref=rows.at[pl.ds(0, count - 1)],
+        dst_ref=rows.at[pl.ds(0, count - 1)],
+        send_sem=row_sem.at[0],
+        recv_sem=row_sem.at[1],
+        device_id={"gx": chip_first + 1 - core},
+        device_id_type=MESH,
+    )
+    all_rows.wait_recv()
+    total = jnp.sum(rows[...], axis=0)
 
     for field in range(3):
         base = FIELD_LANES * field
@@ -244,7 +317,8 @@
             row = row * (jnp.float32(planes) / (jnp.float32(planes) - lag))
         out_ref[field : field + 1, :] = row
 
-    for copy in u_copies + v_copies + d_copies + copies_gx + copies_gy:
+    all_rows.wait_send()
+    for copy in list(u_copies.values()) + v_copies + d_copies:
         copy.wait_send()
 
 
@@ -266,8 +340,7 @@
             pltpu.VMEM((2, quarter, 4, width_x, width_y), jnp.float32),
             pltpu.VMEM((3, half, width_x, width_y), jnp.float32),
             pltpu.SMEM((3, seps), jnp.int32),
-            pltpu.VMEM((n_gx, 1, LANES), jnp.float32),
-            pltpu.VMEM((n_gy, 1, LANES), jnp.float32),
+            pltpu.VMEM((n_gx * n_gy, 1, LANES), jnp.float32),
             dma((3,)),
             dma((3,)),
             dma((3,)),
@@ -277,10 +350,9 @@
             dma((2,)),
             dma((2, half)),
             dma((2, half)),
-            dma((n_gx,)),
-            dma((n_gx,)),
-            dma((n_gy,)),
-            dma((n_gy,)),
+            dma((2,)),
+            pltpu.SemaphoreType.REGULAR((2,)),
+            pltpu.SemaphoreType.REGULAR((n_gy // 2,)),
         ],
         compiler_params=pltpu.CompilerParams(collective_id=0, has_side_effects=True),
     )(u_field, v_field, w_field, sep_x, sep_y, sep_z)

time: 29.1 us -> 25.4 us (0.87)
  Pallas kernels: 27.6 us -> 23.9 us
    pallas_call x1, Pallas kernels: 27.6 us -> 23.9 us  [local(): pl.pallas_call(functools.partial(kernel, n_gx, n_gy), out_shape=jax.Shape...]
where the time goes in v2:
time: 25.4 us; the launch traced here: 25.2 us
  Pallas kernels  23.9 us (94%)
  local copies, waits for them, and re-layouts  1.26 us (5%)
    pallas_call x1, Pallas kernels, local(): pl.pallas_call(functools.partial(kernel, n_gx, n_gy), out_shape=jax.Shape...  23.9 us
    unnamed x1, local copies, waits for them, and re-layouts  1.26 us

profile of v2, /device:TPU:0, one launch (start us, length us, event | category | flops | bytes accessed | tf_op | source)
XLA Modules:
  0.0 25.2 jit_solution(9492497284789706224)
XLA Ops:
  0.0 23.9 %shard_map.64 = f32[3,16]{1,0:T(4,128)} custom-call(f32[8,64,256]{2,1,0:T(8,128)} %u_hbm.1, f32[8,64,256]{2,1,0:T(8,128)} %v_hbm.1, f32[8,64,256]{2,1,0:T(8,128)} %w_hbm.1, s32[16]{0:T(128)} %sep_x_hbm.1, s32[16]{0:T(128)} %sep_y_hbm.1, s32[16]{0:T(128)} %sep_z_hbm.1), custom_call_target="tpu_custom_call" | custom-call | tf_op jit(solution)/shard_map/pallas_call | solution.py:331
  24.0 1.3 %copy.8 = f32[3,16]{1,0:T(4,128)} copy(f32[3,16]{1,0:T(4,128)} %shard_map.64) | data formatting | bytes 384

commit v3 on v2

--- a/solution.py
+++ b/solution.py
@@ -44,7 +44,7 @@
     n_gx, n_gy,
     u_hbm, v_hbm, w_hbm, sep_x_hbm, sep_y_hbm, sep_z_hbm, out_ref,
     u_own, v_own, w_own, u_wide, v_wide, sep_s, rows,
-    load_sem, sep_sem, place_sem, u_send, u_recv, d_send, d_recv, v_send, v_recv,
+    plane_sem, load_sem, sep_sem, place_sem, u_send, u_recv, d_send, d_recv, v_send, v_recv,
     row_sem, line_sem, pair_sem,
 ):
     planes, width_x, width_y = u_own.shape
@@ -54,10 +54,15 @@
     core, parity = lax.rem(gx, 2), lax.rem(gy, 2)
     chip_first = gx - core
 
-    load_u = pltpu.make_async_copy(u_hbm, u_own, load_sem.at[0])
-    load_v = pltpu.make_async_copy(v_hbm, v_own, load_sem.at[1])
-    load_w = pltpu.make_async_copy(w_hbm, w_own, load_sem.at[2])
-    load_u.start()
+    order = [quarter * part + item for item in range(quarter) for part in range(4)]
+    load_u = {
+        plane: pltpu.make_async_copy(u_hbm.at[plane], u_own.at[plane], plane_sem.at[plane])
+        for plane in order
+    }
+    load_v = pltpu.make_async_copy(v_hbm, v_own, load_sem.at[0])
+    load_w = pltpu.make_async_copy(w_hbm, w_own, load_sem.at[1])
+    for plane in order:
+        load_u[plane].start()
     load_v.start()
 
     chip, chips = gx // 2, n_gx // 2
@@ -143,8 +148,8 @@
             device_id_type=MESH,
         ))
 
-    load_u.wait()
-    load_v.wait()
+    for plane in order[:4]:
+        load_u[plane].wait()
     inner = jnp.where(first, 0, 2) + jnp.where(last, 0, 2)
     pl.semaphore_wait(barrier, inner + 3)
 
@@ -159,6 +164,9 @@
 
     for side in range(2):
         start_u(side, range(1), False)
+    for plane in order[4:]:
+        load_u[plane].wait()
+    load_v.wait()
     for copy in v_copies + d_copies:
         copy.start()
 
@@ -282,8 +290,14 @@
     me = gx * n_gy + gy
     rows[me] = mine
 
+    flips = [(1 - 2 * lax.rem(me // (1 << bit), 2)) * (1 << bit) for bit in range(count.bit_length() - 1)]
+    by_flips = count == 1 << len(flips)
+
     def to_device(step):
-        peer = lax.rem(me + step, count)
+        if by_flips and isinstance(step, int):
+            peer = me + sum(flip for bit, flip in enumerate(flips) if step >> bit & 1)
+        else:
+            peer = lax.rem(me + step, count)
         return pltpu.make_async_remote_copy(
             src_ref=rows.at[me],
             dst_ref=rows.at[me],
@@ -294,7 +308,7 @@
         )
 
     if count <= 64:
-        for step in range(1, count):
+        for step in reversed(range(1, count)):
             to_device(step).start()
     else:
         lax.fori_loop(1, count, lambda step, _: to_device(step).start(), None)
@@ -330,7 +344,7 @@
     block = (planes, width_x, width_y)
     return pl.pallas_call(
         functools.partial(kernel, n_gx, n_gy),
-        out_shape=jax.ShapeDtypeStruct((3, seps), jnp.float32),
+        out_shape=pltpu.VMEM((3, seps), jnp.float32),
         in_specs=[pl.BlockSpec(memory_space=pl.ANY)] * 6,
         out_specs=pl.BlockSpec(memory_space=pltpu.VMEM),
         scratch_shapes=[
@@ -341,7 +355,8 @@
             pltpu.VMEM((3, half, width_x, width_y), jnp.float32),
             pltpu.SMEM((3, seps), jnp.int32),
             pltpu.VMEM((n_gx * n_gy, 1, LANES), jnp.float32),
-            dma((3,)),
+            dma((planes,)),
+            dma((2,)),
             dma((3,)),
             dma((3,)),
             dma((2, quarter, 2)),

time: 25.4 us -> 24.2 us (0.953)
  local copies, waits for them, and re-layouts: 1.26 us -> 0.58 us
  Pallas kernels: 23.9 us -> 23.4 us
    unnamed x1, local copies, waits for them, and re-layouts: 1.26 us -> 0.58 us
    pallas_call x1, Pallas kernels: 23.9 us -> 23.4 us  [local(): pl.pallas_call(functools.partial(kernel, n_gx, n_gy), out_shape=pltpu.VME...]
where the time goes in v3:
time: 24.2 us; the launch traced here: 24 us
  Pallas kernels  23.4 us (97%)
  local copies, waits for them, and re-layouts  0.58 us (2%)
    pallas_call x1, Pallas kernels, local(): pl.pallas_call(functools.partial(kernel, n_gx, n_gy), out_shape=pltpu.VME...  23.4 us
    unnamed x1, local copies, waits for them, and re-layouts  0.58 us

profile of v3, /device:TPU:0, one launch (start us, length us, event | category | flops | bytes accessed | tf_op | source)
XLA Modules:
  0.0 24.0 jit_solution(8004832415915878114)
XLA Ops:
  0.0 23.4 %shard_map.64 = f32[3,16]{1,0:T(4,128)S(1)} custom-call(f32[8,64,256]{2,1,0:T(8,128)} %u_hbm.1, f32[8,64,256]{2,1,0:T(8,128)} %v_hbm.1, f32[8,64,256]{2,1,0:T(8,128)} %w_hbm.1, s32[16]{0:T(128)} %sep_x_hbm.1, s32[16]{0:T(128)} %sep_y_hbm.1, s32[16]{0:T(128)} %sep_z_hbm.1), custom_call_target="tpu_custom_call" | custom-call | tf_op jit(solution)/shard_map/pallas_call | solution.py:345
  23.5 0.6 %copy.8 = f32[3,16]{1,0:T(4,128)} copy(f32[3,16]{1,0:T(4,128)S(1)} %shard_map.64) | data formatting | bytes 384

commit v4 on v3

--- a/solution.py
+++ b/solution.py
@@ -162,10 +162,17 @@
                 for other in range(2):
                     u_copies[side, item, other].start()
 
+    ends = first | last
     for side in range(2):
         start_u(side, range(1), False)
     for plane in order[4:]:
         load_u[plane].wait()
+    @pl.when(~ends)
+    def _():
+        for side in range(2):
+            for item in range(1, quarter):
+                for other in range(2):
+                    u_copies[side, item, other].start()
     load_v.wait()
     for copy in v_copies + d_copies:
         copy.start()
@@ -198,8 +205,10 @@
 
     for side in range(2):
         start_u(side, range(quarter), True)
-    for side in range(2):
-        start_u(side, range(1, quarter), False)
+    @pl.when(ends)
+    def _():
+        for side in range(2):
+            start_u(side, range(1, quarter), False)
 
     greet(pair_sem.at[0], gy=near)
     pl.semaphore_wait(pair_sem.at[0], 1)
@@ -262,7 +271,7 @@
     gram_0 = product(left, left, ((0,), (0,)))
     gram_1 = product(left, (high[cells:], low[cells:]), ((0,), (0,)))
     gram_y = jnp.concatenate([gram_0, gram_1], axis=1)
-    part = pick(diagonal_sums(gram_y, width_y), pick_y)
+    rest = jnp.sum(pick(diagonal_sums(gram_y, width_y), pick_y), axis=0, keepdims=True) + row_z
 
     for copy in d_copies:
         copy.wait_recv()
@@ -283,8 +292,7 @@
             lower = (pair[0][: 2 * width_x], pair[1][: 2 * width_x])
             term = product(lower, pair, ((1,), (1,)))
             gram_x = term if gram_x is None else gram_x + term
-    part = part + pick(diagonal_sums(gram_x, 2 * width_x), pick_x)
-    mine = jnp.sum(part, axis=0, keepdims=True) + row_z
+    mine = jnp.sum(pick(diagonal_sums(gram_x, 2 * width_x), pick_x), axis=0, keepdims=True) + rest
 
     count = n_gx * n_gy
     me = gx * n_gy + gy

time: 24.2 us -> 24.2 us (level)
  no operation moved by 1% of the time
where the time goes in v4:
time: 24.2 us; the launch traced here: 24 us
  Pallas kernels  23.4 us (97%)
  local copies, waits for them, and re-layouts  0.58 us (2%)
    pallas_call x1, Pallas kernels, local(): pl.pallas_call(functools.partial(kernel, n_gx, n_gy), out_shape=pltpu.VME...  23.4 us
    unnamed x1, local copies, waits for them, and re-layouts  0.58 us

profile of v4, /device:TPU:0, one launch (start us, length us, event | category | flops | bytes accessed | tf_op | source)
XLA Modules:
  0.0 24.0 jit_solution(6707488626054753639)
XLA Ops:
  0.0 23.4 %shard_map.64 = f32[3,16]{1,0:T(4,128)S(1)} custom-call(f32[8,64,256]{2,1,0:T(8,128)} %u_hbm.1, f32[8,64,256]{2,1,0:T(8,128)} %v_hbm.1, f32[8,64,256]{2,1,0:T(8,128)} %w_hbm.1, s32[16]{0:T(128)} %sep_x_hbm.1, s32[16]{0:T(128)} %sep_y_hbm.1, s32[16]{0:T(128)} %sep_z_hbm.1), custom_call_target="tpu_custom_call" | custom-call | tf_op jit(solution)/shard_map/pallas_call | solution.py:353
  23.4 0.6 %copy.8 = f32[3,16]{1,0:T(4,128)} copy(f32[3,16]{1,0:T(4,128)S(1)} %shard_map.64) | data formatting | bytes 384
